TPU v7x, 32 devices: a whole 2x2x4 slice. The times are simulated.
32 devices in a mesh: tm: 4 (over y, x), space: 8 (over z, core).
Axes of the slice: x: 2, y: 2, z: 4, core: 2. Of those that a mesh axis runs over, the one named last changes fastest.
Arguments:
- fields: bfloat16 [4096, 2, 16384], P('tm', None, 'space')
- calendar_day: int32 [4096], P('tm'), may hold values from 0 to 364, as said below
- events: int32 [16, 96], replicated, may hold values from 0 to 4080, as said below
- lag_offsets: int32 [16], replicated, may hold values from 0 to 15, each once
Outputs:
- composite: float32 [16, 16, 2, 16384], P('tm', None, None, 'space')
Inputs may be any that keep to these rules, and one draw needn't show every extreme that they name: `calendar_day`: days of the year of successive record days, one or two calendar days apart. `events`: each entry is a record day; a day may repeat within a type. `lag_offsets`: each of 0 to 15 once.
All inputs are finite; a program needn't handle non-finite values.
Results may differ from a plain program's by a relative error of at most 0.0012.
Values may be sent and summed in bfloat16 or wider, within the bound.
A program may use at most 64 MiB of HBM per device.

v0:
```python
import jax
import jax.numpy as jnp
from jax import lax
from jax.sharding import PartitionSpec as P

HARMONICS = 4


TWO_PI = 6.283185307179586


def regressors(calendar_day):
    phases = calendar_day.astype(jnp.float32) * (TWO_PI / 365.25)
    columns = [jnp.ones_like(phases)]
    for harmonic in range(1, HARMONICS + 1):
        columns.append(jnp.cos(harmonic * phases))
        columns.append(jnp.sin(harmonic * phases))
    return jnp.stack(columns, axis=1).astype(jnp.bfloat16)


def solve_fit(gram_matrix, projection):
    factor = jnp.linalg.cholesky(gram_matrix)
    return jax.scipy.linalg.cho_solve((factor, True), projection)


def fit_coefficients(gram_matrix, projection):
    gram_matrix, projection = lax.psum((gram_matrix, projection), "tm")
    return solve_fit(gram_matrix, projection)


def day_counts(events, lag_offsets, first_day, length):
    lag_count = lag_offsets.shape[0]
    day_numbers = first_day - (lag_count - 1) + lax.iota(jnp.int32, length + lag_count - 1)

    def type_histogram(event_row):
        matches = event_row[:, None] == day_numbers[None, :]
        return jnp.sum(matches.astype(jnp.float32), axis=0)

    histogram = lax.map(type_histogram, events).astype(jnp.bfloat16)
    shifted = jnp.stack(
        [
            lax.slice_in_dim(
                histogram, lag_count - 1 - offset, lag_count - 1 - offset + length, axis=1
            )
            for offset in range(lag_count)
        ]
    )
    lag_select = (lag_offsets[:, None] == lax.iota(jnp.int32, lag_count)[None, :]).astype(
        jnp.bfloat16
    )
    counts = jnp.einsum("ls,set->elt", lag_select, shifted, preferred_element_type=jnp.float32)
    return counts.astype(jnp.bfloat16).reshape(-1, length)


def shards(fields, calendar_day, events, lag_offsets):
    members = events.shape[1]
    lag_count = lag_offsets.shape[0]
    local_days = fields.shape[0]
    local_points = fields.shape[2]
    record = fields.reshape(local_days, 2 * local_points)
    design = regressors(calendar_day)
    gram_matrix = jnp.dot(design.T, design, preferred_element_type=jnp.float32)
    projection = jnp.dot(design.T, record, preferred_element_type=jnp.float32)
    counts = day_counts(events, lag_offsets, lax.axis_index("tm") * local_days, local_days)
    counted_design = jnp.dot(counts, design, preferred_element_type=jnp.float32)
    coefficients = fit_coefficients(gram_matrix, projection)
    raw_part = jnp.dot(counts, record, preferred_element_type=jnp.float32)
    totals = lax.psum_scatter(
        raw_part - jnp.dot(counted_design, coefficients, precision=lax.Precision.HIGHEST),
        "tm",
        scatter_dimension=0,
        tiled=True,
    )
    maps = (totals / members).reshape(-1, lag_count, 2, local_points)
    map_sums = lax.psum(jnp.sum(maps, axis=3, keepdims=True), "space")
    return maps - map_sums / (local_points * lax.axis_size("space"))


def solution(mesh):
    return jax.shard_map(
        shards,
        mesh=mesh,
        in_specs=(P("tm", None, "space"), P("tm"), P(), P()),
        out_specs=P("tm", None, None, "space"),
        check_vma=False,
    )
```

profile of v0, /device:TPU:0, one launch (start us, length us, event | category | flops | bytes accessed | tf_op | source)
XLA Modules:
  0.0 158.4 jit_solution(3301992195058840388)
XLA Ops:
  6.5 12.0 %copy.372 = bf16[128,8,2,2048]{3,1,2,0:T(8,128)(2,1)} copy(bf16[128,8,2,2048]{3,2,1,0:T(2,128)(2,1)} %bitcast.75) | data formatting | bytes 16777216
  18.8 5.3 %fusion.14 = f32[9,4096]{1,0:T(8,128)} fusion(bf16[1024,9]{0,1:T(8,128)(2,1)S(1)} %stack.112, bf16[1024,4096]{1,0:T(8,128)(2,1)} %bitcast.73), kind=kOutput, calls=%fused_computation.55 | convolution fusion | flops 75497472 | bytes 8554496 | tf_op jit(solution)/shard_map/dot_general | solution.py:63
  24.4 15.2 %while.11 = (s32[]{:T(128)}, bf16[16,1039]{1,0:T(8,128)(2,1)S(1)}, s32[16,96]{1,0:T(8,128)}, s32[]{:T(128)}, s32[]{:T(128)}, /*index=5*/s32[]{:T(128)}) while((s32[]{:T(128)}, bf16[16,1039]{1,0:T(8,128)(2,1)S(1)}, s32[16,96]{1,0:T(8,128)}, s32[]{:T(128)}, s32[]{:T(128)}, /*index=5*/s32[]{:T(128)}) %tuple.43), condition=%wide.region_2.3_spmd.clone, body=%wide.region_0.2_spmd.clone.sunk | while | flops 299234 | bytes 19943 | solution.py:39
  24.4 0.7 dynamic-slice_bitcast_fusion.2
  25.1 0.1 convert_reduce_fusion.2
  25.3 0.7 dynamic-slice_bitcast_fusion.2
  26.3 0.7 dynamic-slice_bitcast_fusion.2
  27.2 0.7 dynamic-slice_bitcast_fusion.2
  27.9 0.1 convert_reduce_fusion.2
  28.2 0.7 dynamic-slice_bitcast_fusion.2
  28.9 0.1 convert_reduce_fusion.2
  29.1 0.7 dynamic-slice_bitcast_fusion.2
  30.1 0.7 dynamic-slice_bitcast_fusion.2
  30.8 0.1 convert_reduce_fusion.2
  31.0 0.7 dynamic-slice_bitcast_fusion.2
  31.7 0.1 convert_reduce_fusion.2
  32.0 0.7 dynamic-slice_bitcast_fusion.2
  32.7 0.1 convert_reduce_fusion.2
  32.9 0.7 dynamic-slice_bitcast_fusion.2
  33.6 0.1 convert_reduce_fusion.2
  33.9 0.7 dynamic-slice_bitcast_fusion.2
  34.8 0.7 dynamic-slice_bitcast_fusion.2
  35.5 0.1 convert_reduce_fusion.2
  35.8 0.7 dynamic-slice_bitcast_fusion.2
  36.7 0.7 dynamic-slice_bitcast_fusion.2
  37.7 0.7 dynamic-slice_bitcast_fusion.2
  38.4 0.1 convert_reduce_fusion.2
  38.6 0.7 dynamic-slice_bitcast_fusion.2
  39.5 0.2 slice_bitcast_fusion
  40.7 1.6 %stack.103 = bf16[16,16,1024]{2,0,1:T(8,128)(2,1)S(1)} concatenate(bf16[1,16,1024]{2,0,1:T(2,128)(2,1)S(1)} %copy.350, bf16[1,16,1024]{2,0,1:T(2,128)(2,1)S(1)} %copy.351, bf16[1,16,1024]{2,0,1:T(2,128)(2,1)S(1)} %copy.352, bf16[1,16,1024]{2,0,1:T(2,128)(2,1)S(1)} %copy.353, bf16[1,16,1024]{2,0,1:T(2,128)(2,1)S(1)} %copy.354, bf16[1,16,1024]{2,0,1:T(2,128)(2,1)S(1)} %copy.355, ...), dimensions={0} | concatenate | bytes 1048576 | tf_op jit(solution)/shard_map/stack | solution.py:40
  42.4 0.4 convolution_convert_fusion
  42.7 7.7 %fusion.11 = f32[256,4096]{1,0:T(8,128)} fusion(bf16[256,1024]{1,0:T(8,128)(2,1)S(1)} %bitcast.76, bf16[1024,4096]{1,0:T(8,128)(2,1)} %bitcast.74), kind=kOutput, calls=%fused_computation.52 | convolution fusion | flops 2147483648 | bytes 13107200 | tf_op jit(solution)/shard_map/dot_general | solution.py:67
  50.4 11.7 %psum.21 = f32[9,9]{0,1:T(8,128)S(1)} all-reduce(f32[9,9]{0,1:T(8,128)S(1)} %fusion.13), channel_id=1, replica_groups=mesh['tm'=4,'space'=8] {'tm'}, use_global_device_ids=true, to_apply=%region_3.4 | all-reduce | flops 81 | bytes 648 | tf_op jit(solution)/shard_map/psum | solution.py:27
  62.2 0.8 cholesky.16
  63.1 0.7 compare_reduce_fusion
  63.8 0.7 fusion.2
  64.5 0.7 custom-call.10
  65.2 0.2 fusion.12
  65.5 4.7 %all-reduce.2.cloned.1.call-done = f32[9,4096]{1,0:T(8,128)} async-done(((f32[9,4096]{1,0:T(8,128)}), f32[9,4096]{1,0:T(8,128)}) %all-reduce.2.cloned.1.call-update) | async-done | bytes 147472 | tf_op jit(solution)/shard_map/psum | solution.py:27
  70.1 1.4 fusion.3
  71.5 0.4 fusion.5
  71.8 6.6 %convolution_subtract_fusion = f32[256,4096]{1,0:T(8,128)} fusion(f32[256,4096]{1,0:T(8,128)} %fusion.11, f32[256,9]{0,1:T(8,128)S(1)} %fusion.12, f32[9,4096]{1,0:T(8,128)S(1)} %fusion.5), kind=kOutput, calls=%fused_computation.4 | convolution fusion | flops 114294784 | bytes 8545280 | tf_op jit(solution)/shard_map/dot_general | solution.py:69
  78.5 52.8 %reduce-scatter.2.cloned.1.call-done = f32[64,4096]{1,0:T(8,128)} async-done(((f32[256,4096]{1,0:T(8,128)}), f32[64,4096]{1,0:T(8,128)}) %reduce-scatter.2.cloned.1.call-update) | async-done | bytes 1048592 | tf_op jit(solution)/shard_map/reduce_scatter | solution.py:68
  131.3 1.3 broadcast_multiply_fusion
  132.6 0.9 reshape.28
  133.5 0.4 reduce_sum.18
  133.9 16.2 %psum.23 = f32[4,16,2,1]{1,0,3,2:T(4,128)S(1)} all-reduce(f32[4,16,2,1]{1,0,3,2:T(4,128)S(1)} %bitcast.78), channel_id=1, replica_groups=mesh['tm'=4,'space'=8] {'space'}, use_global_device_ids=true, to_apply=%region_9.10 | all-reduce | flops 128 | bytes 1024 | tf_op jit(solution)/shard_map/psum | solution.py:75
  150.2 1.4 broadcast_subtract_fusion
  (98 shorter events, 3.9 us)
Async XLA Ops:
  6.5 63.6 %all-reduce.2.cloned.1.call-start = ((), (), s32[]{:S(2)}) async-start(), calls=%async_computation.1 | async-start | bytes 524288 | tf_op jit(solution)/shard_map/psum | solution.py:27
  6.5 12.0 %copy-start = (s32[1024]{0:T(1024)S(1)}, s32[1024]{0:T(1024)}, u32[]{:S(2)}) copy-start(s32[1024]{0:T(1024)} %param.7) | copy-start | bytes 12292
  18.8 23.5 %copy-start.1 = (s32[16]{0:T(128)S(1)}, s32[16]{0:T(128)}, u32[]{:S(2)}) copy-start(s32[16]{0:T(128)} %param.9) | copy-start | bytes 196
  24.2 107.1 %reduce-scatter.2.cloned.1.call-start = ((), (), s32[]{:S(2)}) async-start(), calls=%async_computation.2 | async-start | bytes 5242880 | tf_op jit(solution)/shard_map/reduce_scatter | solution.py:68
Sparse Core Ops, SparseCore 0:
  24.3 45.7 all-reduce.1
  78.6 52.6 reduce-scatter.1
where the time goes:
time: 159 us; the launch traced here: 158 us
  waiting for transfers between devices  57.5 us (36%)
  local copies, waits for them, and re-layouts  28.5 us (18%)
  blocking collectives  27.9 us (18%)
  matrix products  22 us (14%)
  between operations  13.7 us (9%)
  other arithmetic  8.3 us (5%)
    reduce_scatter x1, waiting for transfers between devices, shards(): lax.psum_scatter(raw_part - jnp.dot(counted_design, coefficients, precisi...  52.8 us
    psum x1, blocking collectives, shards(): map_sums = lax.psum(jnp.sum(maps, axis=3, keepdims=True), 'space')  16.2 us
    unnamed x5, local copies, waits for them, and re-layouts  12 us
    psum x1, blocking collectives, fit_coefficients(): gram_matrix, projection = lax.psum((gram_matrix, projection), 'tm')  11.7 us
    eq x16, local copies, waits for them, and re-layouts, type_histogram(): matches = event_row[:, None] == day_numbers[None, :]  11.2 us
    dot_general x1, matrix products, shards(): raw_part = jnp.dot(counts, record, preferred_element_type=jnp.float32)  7.7 us
    dot_general x1, matrix products, shards(): jnp.dot(counted_design, coefficients, precision=lax.Precision.HIGHEST)  6.61 us
    dot_general x1, matrix products, shards(): projection = jnp.dot(design.T, record, preferred_element_type=jnp.float32)  5.3 us
  transfers between devices with their start and end apart: 2, of which 2 were waited for; matrix products, arithmetic and copies ran while one was open for 18% of the time, Pallas kernels for 0%

commit v1 on v0

v1 whole, which is shorter than its diff:
```python
import functools

import jax
import jax.numpy as jnp
from jax import lax
from jax.experimental import pallas as pl
from jax.experimental.pallas import tpu as pltpu
from jax.sharding import PartitionSpec as P

HARMONICS = 4
TERMS = 2 * HARMONICS + 1
TWO_PI = 6.283185307179586
PAD = 128
CHUNK = 256
NT = (((1,), (1,)), ((), ()))
TN = (((0,), (0,)), ((), ()))


def regressor_rows(calendar_day):
    phases = jnp.repeat(calendar_day, 2).astype(jnp.float32) * (TWO_PI / 365.25)
    rows = [jnp.ones_like(phases)]
    for harmonic in range(1, HARMONICS + 1):
        rows.append(jnp.cos(harmonic * phases))
        rows.append(jnp.sin(harmonic * phases))
    rows += [jnp.zeros_like(phases)] * (16 - TERMS)
    return jnp.stack(rows, axis=0).astype(jnp.bfloat16)


def prepare(days_ref, design_ref, weights_ref, normal_ref):
    members, types = days_ref.shape
    depth = design_ref.shape[1]
    shifts = (weights_ref.shape[0] - 32) // types
    places = lax.broadcasted_iota(jnp.int32, (members, depth + PAD), 1) - PAD
    for kind in range(types):
        hits = (days_ref[:, kind : kind + 1] == places).astype(jnp.float32)
        histogram = jnp.sum(hits, axis=0, keepdims=True)
        wide = jnp.broadcast_to(histogram, (shifts, depth + PAD))
        rolled = pltpu.roll(wide, 0, 1, stride=1, stride_axis=0)
        weights_ref[kind * shifts : (kind + 1) * shifts, :] = rolled[:, PAD:].astype(jnp.bfloat16)
    design = design_ref[...]
    odd = lax.broadcasted_iota(jnp.int32, design.shape, 1) % 2
    wide_design = design.astype(jnp.float32)
    weights_ref[types * shifts : types * shifts + 16, :] = jnp.where(odd == 0, wide_design, 0.0).astype(jnp.bfloat16)
    weights_ref[types * shifts + 16 :, :] = jnp.where(odd == 1, wide_design, 0.0).astype(jnp.bfloat16)
    normal_ref[...] = lax.dot_general(design, weights_ref[...], NT, preferred_element_type=jnp.float32)


def split3(value):
    high = value.astype(jnp.bfloat16)
    rest = value - high.astype(jnp.float32)
    middle = rest.astype(jnp.bfloat16)
    low = (rest - middle.astype(jnp.float32)).astype(jnp.bfloat16)
    return high, middle, low


def compose(
    tm, space, members, all_points,
    fields, weights_ref, normal_ref, out_ref,
    xs, normals, left, whole, owned, codes, scales, got_codes, got_scales, sums, got_sums,
    x_sems, n_send, n_recv, c_send, c_recv, s_send, s_recv, m_send, m_recv,
):
    rows = out_ref.shape[0]
    chunks = xs.shape[0]
    count_rows = weights_ref.shape[0] - 32
    me = lax.axis_index("tm")
    here = lax.axis_index("space")

    def load(c):
        return pltpu.make_async_copy(
            fields.at[:, :, pl.ds(pl.multiple_of(c * CHUNK, CHUNK), CHUNK)], xs.at[c], x_sems.at[c]
        )

    lax.fori_loop(0, chunks, lambda c, _: (load(c).start(), 0)[1], 0)

    barrier = pltpu.get_barrier_semaphore()
    for i in range(1, tm):
        pl.semaphore_signal(barrier, inc=1, device_id={"tm": lax.rem(me + i, tm)})
    for i in range(1, space):
        pl.semaphore_signal(barrier, inc=1, device_id={"space": lax.rem(here + i, space)})
    pl.semaphore_wait(barrier, tm + space - 2)

    def send_normal(i):
        return pltpu.make_async_remote_copy(
            normal_ref, normals.at[i - 1], n_send.at[i - 1], n_recv.at[i - 1], device_id={"tm": lax.rem(me + i, tm)}
        )

    def send_code(i, c):
        peer = {"tm": lax.rem(me + i, tm)}
        return (
            pltpu.make_async_remote_copy(
                codes.at[i - 1, c], got_codes.at[i - 1, c], c_send.at[i - 1, c], c_recv.at[i - 1, c], device_id=peer
            ),
            pltpu.make_async_remote_copy(
                scales.at[i - 1, c], got_scales.at[i - 1, c], s_send.at[i - 1, c], s_recv.at[i - 1, c], device_id=peer
            ),
        )

    def send_sums(i):
        return pltpu.make_async_remote_copy(
            sums, got_sums.at[i - 1], m_send.at[i - 1], m_recv.at[i - 1],
            device_id={"space": lax.rem(here + i, space)},
        )

    for i in range(1, tm):
        send_normal(i).start()
    system = normal_ref[...]
    for i in range(1, tm):
        send_normal(i).wait()
        system = system + normals[i - 1]
    lines = lax.broadcasted_iota(jnp.int32, system.shape, 0)
    for k in range(TERMS):
        pivot = system[k : k + 1, :] / system[k : k + 1, count_rows + k : count_rows + k + 1]
        system = jnp.where(lines == k, pivot, system - system[:, count_rows + k : count_rows + k + 1] * pivot)
    fit = system[:, :count_rows]
    fit = jnp.where(lax.broadcasted_iota(jnp.int32, fit.shape, 0) < TERMS, fit, 0.0)
    odd = lax.broadcasted_iota(jnp.int32, fit.shape, 1) % 2
    fit = jnp.concatenate([jnp.where(odd == 0, fit, 0.0), jnp.where(odd == 1, fit, 0.0)], axis=0)
    high, middle, low = split3(fit)
    left[...] = jnp.concatenate([high, high, high, middle, middle, low], axis=0)

    def step(c, _):
        load(c).wait()
        block = xs[c].reshape(weights_ref.shape[1], CHUNK)
        raw = jnp.dot(weights_ref[...], block, preferred_element_type=jnp.float32)
        p_high, p_middle, p_low = split3(raw[count_rows:])
        right = jnp.concatenate([p_high, p_middle, p_low, p_high, p_middle, p_high], axis=0)
        whole[...] = raw[:count_rows] - lax.dot_general(left[...], right, TN, preferred_element_type=jnp.float32)
        for i in range(1, tm):
            peer = lax.rem(me + i, tm)
            part = whole[pl.ds(pl.multiple_of(peer * rows, rows), rows), :]
            top = jnp.max(jnp.abs(part), axis=0, keepdims=True)
            factor = jnp.where(top > 0.0, 32767.0 / jnp.where(top > 0.0, top, 1.0), 0.0)
            codes[i - 1, c] = jnp.round(part * factor).astype(jnp.int32).astype(jnp.int16)
            scales[i - 1, c] = top * (1.0 / 32767.0)
            for copy in send_code(i, c):
                copy.start()
        owned[c] = whole[pl.ds(pl.multiple_of(me * rows, rows), rows), :]
        return 0

    lax.fori_loop(0, chunks, step, 0)

    ones = jnp.ones((8, CHUNK), jnp.bfloat16)

    def gather(c, total):
        value = owned[c]
        for i in range(1, tm):
            for copy in send_code(i, c):
                copy.wait()
            value = value + got_codes[i - 1, c].astype(jnp.int32).astype(jnp.float32) * got_scales[i - 1, c]
        value = value * (1.0 / members)
        owned[c] = value
        for piece in split3(value):
            total = total + lax.dot_general(ones, piece, NT, preferred_element_type=jnp.float32)
        return total

    sums[...] = lax.fori_loop(0, chunks, gather, jnp.zeros((8, rows), jnp.float32))
    for i in range(1, space):
        send_sums(i).start()
    total = sums[...]
    for i in range(1, space):
        send_sums(i).wait()
        total = total + got_sums[i - 1]
    mean = lax.dot_general(
        total * (1.0 / (8 * all_points)), jnp.ones((8, CHUNK), jnp.float32), TN,
        precision=lax.Precision.HIGHEST, preferred_element_type=jnp.float32,
    )

    def finish(c, _):
        out_ref[:, pl.ds(pl.multiple_of(c * CHUNK, CHUNK), CHUNK)] = owned[c] - mean
        return 0

    lax.fori_loop(0, chunks, finish, 0)


def shards(tm, space, fields, calendar_day, events, lag_offsets):
    types, members = events.shape
    lag_count = lag_offsets.shape[0]
    days, variables, points = fields.shape
    depth = variables * days
    count_rows = types * lag_count * variables
    rows = count_rows // tm
    chunks = points // CHUNK
    places = 2 * (events - lax.axis_index("tm") * days).T
    weights, normal = pl.pallas_call(
        prepare,
        out_shape=(
            jax.ShapeDtypeStruct((count_rows + 32, depth), jnp.bfloat16),
            jax.ShapeDtypeStruct((16, count_rows + 32), jnp.float32),
        ),
        in_specs=[pl.BlockSpec(memory_space=pltpu.VMEM)] * 2,
        out_specs=[pl.BlockSpec(memory_space=pltpu.VMEM)] * 2,
        compiler_params=pltpu.CompilerParams(vmem_limit_bytes=48 * 2**20),
        name="prepare",
    )(places, regressor_rows(calendar_day))
    pairs = (tm - 1, chunks)
    dma = pltpu.SemaphoreType.DMA
    result = pl.pallas_call(
        functools.partial(compose, tm, space, members, points * space),
        out_shape=jax.ShapeDtypeStruct((rows, points), jnp.float32),
        in_specs=[
            pl.BlockSpec(memory_space=pl.ANY),
            pl.BlockSpec(memory_space=pltpu.VMEM),
            pl.BlockSpec(memory_space=pltpu.VMEM),
        ],
        out_specs=pl.BlockSpec(memory_space=pltpu.VMEM),
        scratch_shapes=[
            pltpu.VMEM((chunks, days, variables, CHUNK), jnp.bfloat16),
            pltpu.VMEM((tm - 1, 16, count_rows + 32), jnp.float32),
            pltpu.VMEM((192, count_rows), jnp.bfloat16),
            pltpu.VMEM((count_rows, CHUNK), jnp.float32),
            pltpu.VMEM((chunks, rows, CHUNK), jnp.float32),
            pltpu.VMEM(pairs + (rows, CHUNK), jnp.int16),
            pltpu.VMEM(pairs + (1, CHUNK), jnp.float32),
            pltpu.VMEM(pairs + (rows, CHUNK), jnp.int16),
            pltpu.VMEM(pairs + (1, CHUNK), jnp.float32),
            pltpu.VMEM((8, rows), jnp.float32),
            pltpu.VMEM((space - 1, 8, rows), jnp.float32),
            dma((chunks,)),
            dma((tm - 1,)), dma((tm - 1,)),
            dma(pairs), dma(pairs), dma(pairs), dma(pairs),
            dma((space - 1,)), dma((space - 1,)),
        ],
        compiler_params=pltpu.CompilerParams(
            collective_id=0, has_side_effects=True, vmem_limit_bytes=60 * 2**20
        ),
        name="compose",
    )(fields, weights, normal)
    maps = result.reshape(types // tm, lag_count, variables, points)
    return jnp.take(maps, lag_offsets, axis=1)


def solution(mesh):
    return jax.shard_map(
        functools.partial(shards, mesh.shape["tm"], mesh.shape["space"]),
        mesh=mesh,
        in_specs=(P("tm", None, "space"), P("tm"), P(), P()),
        out_specs=P("tm", None, None, "space"),
        check_vma=False,
    )
```

time: 159 us -> 59.7 us (0.38)
  waiting for transfers between devices: 57.5 us -> 0 us
  Pallas kernels: 0 us -> 45.6 us
  blocking collectives: 27.9 us -> 0 us
  matrix products: 22 us -> 0 us
  local copies, waits for them, and re-layouts: 28.5 us -> 11.9 us
  between operations: 13.7 us -> 0.18 us
  other arithmetic: 8.3 us -> 1.8 us
    reduce_scatter x1 -> x0, waiting for transfers between devices: 52.8 us -> none  [shards(): lax.psum_scatter(raw_part - jnp.dot(counted_design, coefficients, precisi...]
    pallas_call x0 -> x2, Pallas kernels: none -> 45.6 us  [the longest x1 42.6 us: shards(): pl.pallas_call(functools.partial(compose, tm, space, members, points * sp...]
    psum x2 -> x0, blocking collectives: 27.9 us -> none  [the longest x1 16.2 us: shards(): map_sums = lax.psum(jnp.sum(maps, axis=3, keepdims=True), 'space')]
    dot_general x6 -> x0, matrix products: 20.3 us -> none  [the longest x1 7.7 us: shards(): raw_part = jnp.dot(counts, record, preferred_element_type=jnp.float32)]
    eq x16 -> x0, local copies, waits for them, and re-layouts: 11.2 us -> none  [type_histogram(): matches = event_row[:, None] == day_numbers[None, :]]
    unnamed x5 -> x6, local copies, waits for them, and re-layouts: 12 us -> 2.02 us
    psum x1 -> x0, waiting for transfers between devices: 4.66 us -> none  [fit_coefficients(): gram_matrix, projection = lax.psum((gram_matrix, projection), 'tm')]
    another operation x28 -> x5, local copies, waits for them, and re-layouts: 2.8 us -> 0.19 us  [regressor_rows(): return jnp.stack(rows, axis=0).astype(jnp.bfloat16)]
  transfers between devices with their start and end apart: 2 -> 0, of which waited for: 2 -> 0; matrix products, arithmetic and copies ran while one was open for 18% -> 0% of each run, Pallas kernels for 0% -> 0%
where the time goes in v1:
time: 59.7 us; the launch traced here: 59.4 us
  Pallas kernels  45.6 us (76%)
  local copies, waits for them, and re-layouts  11.9 us (20%)
  other arithmetic  1.8 us (3%)
    pallas_call x1, Pallas kernels, shards(): pl.pallas_call(functools.partial(compose, tm, space, members, points * sp...  42.6 us
    pallas_call x1, Pallas kernels, shards(): pl.pallas_call(prepare, out_shape=(jax.ShapeDtypeStruct((count_rows + 32,...  2.97 us
    reshape x2, local copies, waits for them, and re-layouts, shards(): maps = result.reshape(types // tm, lag_count, variables, points)  2.55 us
    unnamed x6, local copies, waits for them, and re-layouts  2.02 us
    select_n x1, local copies, waits for them, and re-layouts, shards(): return jnp.take(maps, lag_offsets, axis=1)  1.78 us
    broadcast_in_dim x8, local copies, waits for them, and re-layouts, regressor_rows(): phases = jnp.repeat(calendar_day, 2).astype(jnp.float32) * (TWO_PI / 365.25)  1.6 us
    cos x4, local copies, waits for them, and re-layouts, regressor_rows(): rows.append(jnp.cos(harmonic * phases))  1.22 us
    sin x4, local copies, waits for them, and re-layouts, regressor_rows(): rows.append(jnp.sin(harmonic * phases))  1.22 us

profile of v1, /device:TPU:0, one launch (start us, length us, event | category | flops | bytes accessed | tf_op | source)
XLA Modules:
  0.0 59.4 jit_solution(13675453615610024274)
XLA Ops:
  0.0 0.8 %sine_convert_fusion = (bf16[1024]{0:T(1024)(128)(2,1)S(1)}, bf16[1024]{0:T(1024)(128)(2,1)S(1)}, bf16[1024]{0:T(1024)(128)(2,1)S(1)}, bf16[1024]{0:T(1024)(128)...) fusion(s32[1024]{0:T(1024)} %param.5), kind=kLoop, calls=%fused_computation.4 | loop fusion | flops 13312 | bytes 20480 | tf_op jit(solution)/shard_map/convert.28
  0.8 0.2 broadcast_in_dim.30
  1.0 0.3 cos.57
  1.3 0.2 broadcast_in_dim.32
  1.5 0.3 cos.59
  1.8 0.2 broadcast_in_dim.34
  2.0 0.3 cos.61
  2.3 0.2 broadcast_in_dim.36
  2.5 0.3 cos.63
  2.8 0.2 broadcast_in_dim.31
  3.0 0.3 sin.57
  3.3 0.2 broadcast_in_dim.33
  3.5 0.3 sin.59
  3.8 0.2 broadcast_in_dim.35
  4.1 0.3 sin.61
  4.4 0.0 copy-start.2
  4.4 0.2 broadcast_in_dim.37
  4.6 0.3 sin.63
  4.9 0.2 stack.9.design_ref
  5.1 0.7 %subtract_multiply_fusion = s32[16,96]{1,0:T(8,128)S(1)} fusion(s32[16,96]{1,0:T(8,128)} %param.6, s32[]{:T(128)S(6)} %mul.87), kind=kLoop, calls=%fused_computation.2 | loop fusion | flops 3072 | bytes 12292 | tf_op jit(solution)/shard_map/mul | solution.py:183
  5.8 0.1 copy.13
  5.9 3.0 %prepare.1 = (bf16[544,2048]{1,0:T(8,128)(2,1)S(1)}, f32[16,544]{1,0:T(8,128)S(1)}) custom-call(s32[96,16]{1,0:T(8,128)S(1)} %bitcast.3, bf16[16,2048]{1,0:T(8,128)(2,1)S(1)} %stack.9.design_ref), custom_call_target="tpu_custom_call" | custom-call | tf_op jit(solution)/shard_map/prepare/pallas_call | solution.py:184
  8.9 0.0 copy-start
  8.9 1.4 %copy-done = bf16[544,2048]{1,0:T(8,128)(2,1)} copy-done((bf16[544,2048]{1,0:T(8,128)(2,1)}, bf16[544,2048]{1,0:T(8,128)(2,1)S(1)}, u32[]{:S(2)}) %copy-start) | copy-done | bytes 2228248
  10.3 0.0 copy-start.1
  10.3 0.6 %copy-done.1 = f32[16,544]{1,0:T(8,128)} copy-done((f32[16,544]{1,0:T(8,128)}, f32[16,544]{1,0:T(8,128)S(1)}, u32[]{:S(2)}) %copy-start.1) | copy-done | bytes 34840
  10.9 42.6 %compose.1 = f32[128,2048]{1,0:T(8,128)} custom-call(bf16[1024,2,2048]{2,1,0:T(2,128)(2,1)} %fields.1, bf16[544,2048]{1,0:T(8,128)(2,1)} %copy-done, f32[16,544]{1,0:T(8,128)} %copy-done.1), custom_call_target="tpu_custom_call" | custom-call | tf_op jit(solution)/shard_map/compose/pallas_call | solution.py:197
  53.5 1.8 %reshape.108 = f32[4,16,2,2048]{3,2,1,0:T(2,128)S(1)} reshape(f32[128,2048]{1,0:T(8,128)} %compose.1) | data formatting | bytes 2097152 | tf_op jit(solution)/shard_map/reshape | solution.py:228
  55.4 0.7 %copy.14 = f32[4,16,2,2048]{3,0,2,1:T(4,128)S(1)} copy(f32[4,16,2,2048]{3,2,1,0:T(2,128)S(1)} %reshape.108) | data formatting | bytes 2097152 | tf_op jit(solution)/shard_map/reshape | solution.py:228
  56.1 0.0 copy-done.2
  56.1 1.2 %gather_fusion = f32[16,4,2,2048]{3,1,2,0:T(4,128)S(1)} fusion(f32[4,16,2,2048]{3,0,2,1:T(4,128)S(1)} %copy.14, s32[1024]{0:T(1024)S(1)} %pad_clamp_fusion), kind=kCustom, calls=%fused_computation | custom fusion | bytes 2097216 | tf_op jit(solution)/shard_map/jit(_take)/gather | solution.py:229
  57.3 0.3 select_bitcast_fusion
  57.7 1.8 %copy.15 = f32[4,16,2,2048]{3,2,1,0:T(2,128)} copy(f32[4,16,2,2048]{3,0,2,1:T(4,128)S(1)} %select_bitcast_fusion) | data formatting | bytes 2097152 | tf_op jit(solution)/shard_map/jit(_take)/select_n | solution.py:229
  (7 shorter events, 0.0 us)
Async XLA Ops:
  4.4 51.7 %copy-start.2 = (s32[16]{0:T(128)S(1)}, s32[16]{0:T(128)}, u32[]{:S(2)}) copy-start(s32[16]{0:T(128)} %param.7) | copy-start | bytes 196
  8.9 1.4 %copy-start = (bf16[544,2048]{1,0:T(8,128)(2,1)}, bf16[544,2048]{1,0:T(8,128)(2,1)S(1)}, u32[]{:S(2)}) copy-start(bf16[544,2048]{1,0:T(8,128)(2,1)S(1)} %get-tuple-element.7.weights_ref) | copy-start | bytes 6684676
  10.3 0.6 %copy-start.1 = (f32[16,544]{1,0:T(8,128)}, f32[16,544]{1,0:T(8,128)S(1)}, u32[]{:S(2)}) copy-start(f32[16,544]{1,0:T(8,128)S(1)} %get-tuple-element.8.normal_ref) | copy-start | bytes 104452

commit v2 on v1

--- a/solution.py
+++ b/solution.py
@@ -18,12 +18,11 @@
 
 def regressor_rows(calendar_day):
     phases = jnp.repeat(calendar_day, 2).astype(jnp.float32) * (TWO_PI / 365.25)
-    rows = [jnp.ones_like(phases)]
-    for harmonic in range(1, HARMONICS + 1):
-        rows.append(jnp.cos(harmonic * phases))
-        rows.append(jnp.sin(harmonic * phases))
-    rows += [jnp.zeros_like(phases)] * (16 - TERMS)
-    return jnp.stack(rows, axis=0).astype(jnp.bfloat16)
+    line = lax.iota(jnp.int32, 16)[:, None]
+    angles = ((line + 1) // 2).astype(jnp.float32) * phases[None, :]
+    rows = jnp.where(line % 2 == 1, jnp.cos(angles), jnp.sin(angles))
+    rows = jnp.where(line == 0, 1.0, jnp.where(line < TERMS, rows, 0.0))
+    return rows.astype(jnp.bfloat16)
 
 
 def prepare(days_ref, design_ref, weights_ref, normal_ref):
@@ -53,23 +52,45 @@
     return high, middle, low
 
 
+def encode(part):
+    top = jnp.max(jnp.abs(part), axis=0, keepdims=True)
+    factor = jnp.where(top > 0.0, 32767.0 / jnp.where(top > 0.0, top, 1.0), 0.0)
+    return jnp.round(part * factor).astype(jnp.int32).astype(jnp.int16), top * (1.0 / 32767.0)
+
+
+def decode(codes, scale):
+    return codes.astype(jnp.int32).astype(jnp.float32) * scale
+
+
+def flip(index, bits):
+    bit = 1
+    flipped = index
+    while bit <= bits:
+        if bits & bit:
+            flipped = flipped + bit - 2 * bit * lax.rem(lax.div(index, bit), 2)
+        bit *= 2
+    return flipped
+
+
 def compose(
     tm, space, members, all_points,
-    fields, weights_ref, normal_ref, out_ref,
-    xs, normals, left, whole, owned, codes, scales, got_codes, got_scales, sums, got_sums,
-    x_sems, n_send, n_recv, c_send, c_recv, s_send, s_recv, m_send, m_recv,
+    fields, weights_hbm, normal_ref, out_ref, mean_ref,
+    xs, weights_ref, normals, left, whole, parts, codes, scales, got_codes, got_scales, sums, got_sums,
+    w_sem, x_sems, n_send, n_recv, c_send, c_recv, s_send, s_recv, m_send, m_recv,
 ):
-    rows = out_ref.shape[0]
-    chunks = xs.shape[0]
+    chunks, rows, _ = out_ref.shape
     count_rows = weights_ref.shape[0] - 32
     me = lax.axis_index("tm")
     here = lax.axis_index("space")
+    stages = tm.bit_length() - 1
 
     def load(c):
         return pltpu.make_async_copy(
             fields.at[:, :, pl.ds(pl.multiple_of(c * CHUNK, CHUNK), CHUNK)], xs.at[c], x_sems.at[c]
         )
 
+    load_weights = pltpu.make_async_copy(weights_hbm, weights_ref, w_sem)
+    load_weights.start()
     lax.fori_loop(0, chunks, lambda c, _: (load(c).start(), 0)[1], 0)
 
     barrier = pltpu.get_barrier_semaphore()
@@ -84,14 +105,15 @@
             normal_ref, normals.at[i - 1], n_send.at[i - 1], n_recv.at[i - 1], device_id={"tm": lax.rem(me + i, tm)}
         )
 
-    def send_code(i, c):
-        peer = {"tm": lax.rem(me + i, tm)}
+    def send_code(apart, bit, c):
+        peer = {"tm": flip(me, bit)}
+        d = apart - 1
         return (
             pltpu.make_async_remote_copy(
-                codes.at[i - 1, c], got_codes.at[i - 1, c], c_send.at[i - 1, c], c_recv.at[i - 1, c], device_id=peer
+                codes.at[d, c], got_codes.at[d, c], c_send.at[d, c], c_recv.at[d, c], device_id=peer
             ),
             pltpu.make_async_remote_copy(
-                scales.at[i - 1, c], got_scales.at[i - 1, c], s_send.at[i - 1, c], s_recv.at[i - 1, c], device_id=peer
+                scales.at[d, c], got_scales.at[d, c], s_send.at[d, c], s_recv.at[d, c], device_id=peer
             ),
         )
 
@@ -117,59 +139,93 @@
     fit = jnp.concatenate([jnp.where(odd == 0, fit, 0.0), jnp.where(odd == 1, fit, 0.0)], axis=0)
     high, middle, low = split3(fit)
     left[...] = jnp.concatenate([high, high, high, middle, middle, low], axis=0)
-
-    def step(c, _):
+    load_weights.wait()
+
+    def bits_of(turn):
+        return [1 << ((turn + stage) % stages) for stage in range(stages)]
+
+    def leaving(turn, stage):
+        bits = bits_of(turn)
+        return [
+            apart for apart in range(1, tm)
+            if apart & bits[stage] and not any(apart & bit for bit in bits[:stage])
+        ]
+
+    def each_chunk(body, start):
+        def group(g, carry):
+            for turn in range(stages):
+                carry = body(g * stages + turn, turn, carry)
+            return carry
+
+        return lax.fori_loop(0, chunks // stages, group, start)
+
+    def post(c, turn, stage):
+        for apart in leaving(turn, stage):
+            codes[apart - 1, c], scales[apart - 1, c] = encode(parts[apart, c])
+            for copy in send_code(apart, bits_of(turn)[stage], c):
+                copy.start()
+
+    def collect(c, turn, stage):
+        bit = bits_of(turn)[stage]
+        for apart in leaving(turn, stage):
+            for copy in send_code(apart, bit, c):
+                copy.wait()
+            parts[apart - bit, c] += decode(got_codes[apart - 1, c], got_scales[apart - 1, c])
+
+    def compute(c, turn, carry):
         load(c).wait()
         block = xs[c].reshape(weights_ref.shape[1], CHUNK)
         raw = jnp.dot(weights_ref[...], block, preferred_element_type=jnp.float32)
         p_high, p_middle, p_low = split3(raw[count_rows:])
         right = jnp.concatenate([p_high, p_middle, p_low, p_high, p_middle, p_high], axis=0)
         whole[...] = raw[:count_rows] - lax.dot_general(left[...], right, TN, preferred_element_type=jnp.float32)
-        for i in range(1, tm):
-            peer = lax.rem(me + i, tm)
-            part = whole[pl.ds(pl.multiple_of(peer * rows, rows), rows), :]
-            top = jnp.max(jnp.abs(part), axis=0, keepdims=True)
-            factor = jnp.where(top > 0.0, 32767.0 / jnp.where(top > 0.0, top, 1.0), 0.0)
-            codes[i - 1, c] = jnp.round(part * factor).astype(jnp.int32).astype(jnp.int16)
-            scales[i - 1, c] = top * (1.0 / 32767.0)
-            for copy in send_code(i, c):
-                copy.start()
-        owned[c] = whole[pl.ds(pl.multiple_of(me * rows, rows), rows), :]
-        return 0
-
-    lax.fori_loop(0, chunks, step, 0)
+        for apart in range(tm):
+            parts[apart, c] = whole[pl.ds(pl.multiple_of(flip(me, apart) * rows, rows), rows), :]
+        post(c, turn, 0)
+        return carry
+
+    each_chunk(compute, 0)
+
+    for stage in range(1, stages):
+        def relay(c, turn, carry):
+            collect(c, turn, stage - 1)
+            post(c, turn, stage)
+            return carry
+
+        each_chunk(relay, 0)
 
     ones = jnp.ones((8, CHUNK), jnp.bfloat16)
 
-    def gather(c, total):
-        value = owned[c]
-        for i in range(1, tm):
-            for copy in send_code(i, c):
-                copy.wait()
-            value = value + got_codes[i - 1, c].astype(jnp.int32).astype(jnp.float32) * got_scales[i - 1, c]
-        value = value * (1.0 / members)
-        owned[c] = value
+    def gather(c, turn, total):
+        collect(c, turn, stages - 1)
+        value = parts[0, c] * (1.0 / members)
+        out_ref[c] = value
         for piece in split3(value):
             total = total + lax.dot_general(ones, piece, NT, preferred_element_type=jnp.float32)
         return total
 
-    sums[...] = lax.fori_loop(0, chunks, gather, jnp.zeros((8, rows), jnp.float32))
+    sums[...] = each_chunk(gather, jnp.zeros((8, rows), jnp.float32))
     for i in range(1, space):
         send_sums(i).start()
     total = sums[...]
     for i in range(1, space):
         send_sums(i).wait()
         total = total + got_sums[i - 1]
-    mean = lax.dot_general(
+    mean_ref[...] = lax.dot_general(
         total * (1.0 / (8 * all_points)), jnp.ones((8, CHUNK), jnp.float32), TN,
         precision=lax.Precision.HIGHEST, preferred_element_type=jnp.float32,
     )
 
-    def finish(c, _):
-        out_ref[:, pl.ds(pl.multiple_of(c * CHUNK, CHUNK), CHUNK)] = owned[c] - mean
-        return 0
-
-    lax.fori_loop(0, chunks, finish, 0)
+
+def finish(lags_ref, values_ref, mean_ref, out_ref, natural):
+    chunks = values_ref.shape[0]
+    lag_count = out_ref.shape[1]
+    mean = mean_ref[...]
+    for c in range(chunks):
+        centred = values_ref[c] - mean
+        natural[:, :, c * CHUNK : (c + 1) * CHUNK] = centred.reshape(lag_count, 2, CHUNK)
+    for lag in range(lag_count):
+        out_ref[0, lag] = natural[lags_ref[lag]]
 
 
 def shards(tm, space, fields, calendar_day, events, lag_offsets):
@@ -194,28 +250,32 @@
     )(places, regressor_rows(calendar_day))
     pairs = (tm - 1, chunks)
     dma = pltpu.SemaphoreType.DMA
-    result = pl.pallas_call(
+    values, mean = pl.pallas_call(
         functools.partial(compose, tm, space, members, points * space),
-        out_shape=jax.ShapeDtypeStruct((rows, points), jnp.float32),
+        out_shape=(
+            jax.ShapeDtypeStruct((chunks, rows, CHUNK), jnp.float32),
+            jax.ShapeDtypeStruct((rows, CHUNK), jnp.float32),
+        ),
         in_specs=[
             pl.BlockSpec(memory_space=pl.ANY),
-            pl.BlockSpec(memory_space=pltpu.VMEM),
+            pl.BlockSpec(memory_space=pl.ANY),
             pl.BlockSpec(memory_space=pltpu.VMEM),
         ],
-        out_specs=pl.BlockSpec(memory_space=pltpu.VMEM),
+        out_specs=[pl.BlockSpec(memory_space=pltpu.VMEM)] * 2,
         scratch_shapes=[
             pltpu.VMEM((chunks, days, variables, CHUNK), jnp.bfloat16),
+            pltpu.VMEM((count_rows + 32, depth), jnp.bfloat16),
             pltpu.VMEM((tm - 1, 16, count_rows + 32), jnp.float32),
             pltpu.VMEM((192, count_rows), jnp.bfloat16),
             pltpu.VMEM((count_rows, CHUNK), jnp.float32),
-            pltpu.VMEM((chunks, rows, CHUNK), jnp.float32),
+            pltpu.VMEM((tm, chunks, rows, CHUNK), jnp.float32),
             pltpu.VMEM(pairs + (rows, CHUNK), jnp.int16),
             pltpu.VMEM(pairs + (1, CHUNK), jnp.float32),
             pltpu.VMEM(pairs + (rows, CHUNK), jnp.int16),
             pltpu.VMEM(pairs + (1, CHUNK), jnp.float32),
             pltpu.VMEM((8, rows), jnp.float32),
             pltpu.VMEM((space - 1, 8, rows), jnp.float32),
-            dma((chunks,)),
+            dma, dma((chunks,)),
             dma((tm - 1,)), dma((tm - 1,)),
             dma(pairs), dma(pairs), dma(pairs), dma(pairs),
             dma((space - 1,)), dma((space - 1,)),
@@ -225,8 +285,20 @@
         ),
         name="compose",
     )(fields, weights, normal)
-    maps = result.reshape(types // tm, lag_count, variables, points)
-    return jnp.take(maps, lag_offsets, axis=1)
+    shifts = lag_count * variables
+    return pl.pallas_call(
+        finish,
+        grid=(types // tm,),
+        out_shape=jax.ShapeDtypeStruct((types // tm, lag_count, variables, points), jnp.float32),
+        in_specs=[
+            pl.BlockSpec(memory_space=pltpu.SMEM),
+            pl.BlockSpec((chunks, shifts, CHUNK), lambda kind: (0, kind, 0)),
+            pl.BlockSpec((shifts, CHUNK), lambda kind: (kind, 0)),
+        ],
+        out_specs=pl.BlockSpec((1, lag_count, variables, points), lambda kind: (kind, 0, 0, 0)),
+        scratch_shapes=[pltpu.VMEM((lag_count, variables, points), jnp.float32)],
+        name="finish",
+    )(lag_offsets, values, mean)
 
 
 def solution(mesh):

time: 59.7 us -> 51.2 us (0.86)
  local copies, waits for them, and re-layouts: 11.9 us -> 2.57 us
  Pallas kernels: 45.6 us -> 46.4 us
    pallas_call x0 -> x1, Pallas kernels: none -> 3.54 us  [shards(): pl.pallas_call(finish, grid=(types // tm,), out_shape=jax.ShapeDtypeStruc...]
    pallas_call x1, Pallas kernels: 42.6 us -> 39.9 us  [shards(): pl.pallas_call(functools.partial(compose, tm, space, members, points * sp...]
    reshape x2 -> x0, local copies, waits for them, and re-layouts: 2.55 us -> none  [shards(): maps = result.reshape(types // tm, lag_count, variables, points)]
    select_n x1 -> x0, local copies, waits for them, and re-layouts: 1.78 us -> none  [shards(): return jnp.take(maps, lag_offsets, axis=1)]
    broadcast_in_dim x8 -> x1, local copies, waits for them, and re-layouts: 1.6 us -> 0.19 us  [regressor_rows(): phases = jnp.repeat(calendar_day, 2).astype(jnp.float32) * (TWO_PI / 365.25)]
    cos x4 -> x0, local copies, waits for them, and re-layouts: 1.22 us -> none  [regressor_rows(): rows.append(jnp.cos(harmonic * phases))]
    sin x4 -> x0, local copies, waits for them, and re-layouts: 1.22 us -> none  [regressor_rows(): rows.append(jnp.sin(harmonic * phases))]
    gather x1 -> x0, local copies, waits for them, and re-layouts: 1.17 us -> none  [shards(): return jnp.take(maps, lag_offsets, axis=1)]
where the time goes in v2:
time: 51.2 us; the launch traced here: 50.9 us
  Pallas kernels  46.4 us (91%)
  local copies, waits for them, and re-layouts  2.57 us (5%)
  other arithmetic  1.96 us (4%)
    pallas_call x1, Pallas kernels, shards(): pl.pallas_call(functools.partial(compose, tm, space, members, points * sp...  39.9 us
    pallas_call x1, Pallas kernels, shards(): pl.pallas_call(finish, grid=(types // tm,), out_shape=jax.ShapeDtypeStruc...  3.54 us
    pallas_call x1, Pallas kernels, shards(): pl.pallas_call(prepare, out_shape=(jax.ShapeDtypeStruct((count_rows + 32,...  2.97 us
    unnamed x4, local copies, waits for them, and re-layouts  2.02 us

profile of v2, /device:TPU:0, one launch (start us, length us, event | category | flops | bytes accessed | tf_op | source)
XLA Modules:
  0.0 50.9 jit_solution(14636273338987202958)
XLA Ops:
  0.0 0.7 %convert_multiply_fusion = f32[1024]{0:T(1024)S(1)} fusion(s32[1024]{0:T(1024)} %param.5), kind=kLoop, calls=%fused_computation.7 | loop fusion | flops 2048 | bytes 8192 | tf_op jit(solution)/shard_map/mul | solution.py:20
  0.7 0.7 %subtract_multiply_fusion = s32[16,96]{1,0:T(8,128)S(1)} fusion(s32[16,96]{1,0:T(8,128)} %param.6, s32[]{:T(128)S(6)} %mul.38), kind=kLoop, calls=%fused_computation.6 | loop fusion | flops 3072 | bytes 12292 | tf_op jit(solution)/shard_map/mul | solution.py:239
  1.4 0.1 copy.11
  1.5 0.2 broadcast_in_dim.41
  1.7 0.3 mul.45
  2.0 0.6 %fusion.3.design_ref = bf16[16,2048]{1,0:T(8,128)(2,1)S(1)} fusion(f32[2048]{0:T(1024)S(1)} %mul.45, f32[16]{0:T(128)S(1)} %fusion.5, pred[16]{0:T(512)(128)(4,1)S(1)} %get-tuple-element.13, pred[16]{0:T(512)(128)(4,1)S(1)} %get-tuple-element.14, pred[16]{0:T(512)(128)(4,1)S(1)} %iota_compare_fusion.1), kind=kLoop, calls=%fused_computation.5 | loop fusion | flops 163840 | bytes 73840 | tf_op jit(solution)/shard_map/convert_element_type | solution.py:25
  2.5 3.0 %prepare.1 = (bf16[544,2048]{1,0:T(8,128)(2,1)S(1)}, f32[16,544]{1,0:T(8,128)S(1)}) custom-call(s32[96,16]{1,0:T(8,128)S(1)} %bitcast.1, bf16[16,2048]{1,0:T(8,128)(2,1)S(1)} %fusion.3.design_ref), custom_call_target="tpu_custom_call" | custom-call | tf_op jit(solution)/shard_map/prepare/pallas_call | solution.py:240
  5.5 0.0 copy-start
  5.5 1.4 %copy-done = bf16[544,2048]{1,0:T(8,128)(2,1)} copy-done((bf16[544,2048]{1,0:T(8,128)(2,1)}, bf16[544,2048]{1,0:T(8,128)(2,1)S(1)}, u32[]{:S(2)}) %copy-start) | copy-done | bytes 2228248
  6.9 0.0 copy-start.1
  6.9 0.6 %copy-done.1 = f32[16,544]{1,0:T(8,128)} copy-done((f32[16,544]{1,0:T(8,128)}, f32[16,544]{1,0:T(8,128)S(1)}, u32[]{:S(2)}) %copy-start.1) | copy-done | bytes 34840
  7.5 39.9 %compose.1 = (f32[8,128,256]{2,1,0:T(8,128)}, f32[128,256]{1,0:T(8,128)}) custom-call(bf16[1024,2,2048]{2,1,0:T(2,128)(2,1)} %fields.1, bf16[544,2048]{1,0:T(8,128)(2,1)} %copy-done, f32[16,544]{1,0:T(8,128)} %copy-done.1), custom_call_target="tpu_custom_call" | custom-call | tf_op jit(solution)/shard_map/compose/pallas_call | solution.py:253
  47.4 3.5 %finish.1 = f32[4,16,2,2048]{3,2,1,0:T(2,128)} custom-call(s32[16]{0:T(128)} %lags_ref.1, f32[8,128,256]{2,1,0:T(8,128)} %get-tuple-element.11.values_ref, f32[128,256]{1,0:T(8,128)} %get-tuple-element.12.mean_ref), custom_call_target="tpu_custom_call" | custom-call | tf_op jit(solution)/shard_map/finish/pallas_call | solution.py:289
  (3 shorter events, 0.0 us)
Async XLA Ops:
  5.5 1.4 %copy-start = (bf16[544,2048]{1,0:T(8,128)(2,1)}, bf16[544,2048]{1,0:T(8,128)(2,1)S(1)}, u32[]{:S(2)}) copy-start(bf16[544,2048]{1,0:T(8,128)(2,1)S(1)} %get-tuple-element.9.weights_hbm) | copy-start | bytes 6684676
  6.9 0.6 %copy-start.1 = (f32[16,544]{1,0:T(8,128)}, f32[16,544]{1,0:T(8,128)S(1)}, u32[]{:S(2)}) copy-start(f32[16,544]{1,0:T(8,128)S(1)} %get-tuple-element.10.normal_ref) | copy-start | bytes 104452

commit v3 on v2

--- a/solution.py
+++ b/solution.py
@@ -281,7 +281,7 @@
             dma((space - 1,)), dma((space - 1,)),
         ],
         compiler_params=pltpu.CompilerParams(
-            collective_id=0, has_side_effects=True, vmem_limit_bytes=60 * 2**20
+            collective_id=0, has_side_effects=True, vmem_limit_bytes=48 * 2**20
         ),
         name="compose",
     )(fields, weights, normal)
@@ -297,6 +297,7 @@
         ],
         out_specs=pl.BlockSpec((1, lag_count, variables, points), lambda kind: (kind, 0, 0, 0)),
         scratch_shapes=[pltpu.VMEM((lag_count, variables, points), jnp.float32)],
+        compiler_params=pltpu.CompilerParams(vmem_limit_bytes=40 * 2**20),
         name="finish",
     )(lag_offsets, values, mean)
 

time: 51.2 us -> 46.8 us (0.914)
  Pallas kernels: 46.4 us -> 44 us
  local copies, waits for them, and re-layouts: 2.57 us -> 0.56 us
    unnamed x4 -> x2, local copies, waits for them, and re-layouts: 2.02 us -> 0.01 us
    pallas_call x1, Pallas kernels: 3.54 us -> 2.3 us  [shards(): pl.pallas_call(finish, grid=(types // tm,), out_shape=jax.ShapeDtypeStruc...]
    pallas_call x1, Pallas kernels: 39.9 us -> 38.8 us  [shards(): pl.pallas_call(functools.partial(compose, tm, space, members, points * sp...]
where the time goes in v3:
time: 46.8 us; the launch traced here: 46.6 us
  Pallas kernels  44 us (94%)
  other arithmetic  1.96 us (4%)
  local copies, waits for them, and re-layouts  0.56 us (1%)
    pallas_call x1, Pallas kernels, shards(): pl.pallas_call(functools.partial(compose, tm, space, members, points * sp...  38.8 us
    pallas_call x1, Pallas kernels, shards(): pl.pallas_call(prepare, out_shape=(jax.ShapeDtypeStruct((count_rows + 32,...  2.98 us
    pallas_call x1, Pallas kernels, shards(): pl.pallas_call(finish, grid=(types // tm,), out_shape=jax.ShapeDtypeStruc...  2.3 us

profile of v3, /device:TPU:0, one launch (start us, length us, event | category | flops | bytes accessed | tf_op | source)
XLA Modules:
  0.0 46.6 jit_solution(2727560769243494252)
XLA Ops:
  0.0 0.0 copy-start
  0.0 0.7 %convert_multiply_fusion = f32[1024]{0:T(1024)S(1)} fusion(s32[1024]{0:T(1024)} %param.5), kind=kLoop, calls=%fused_computation.7 | loop fusion | flops 2048 | bytes 8192 | tf_op jit(solution)/shard_map/mul | solution.py:20
  0.7 0.7 %subtract_multiply_fusion = s32[16,96]{1,0:T(8,128)S(1)} fusion(s32[16,96]{1,0:T(8,128)} %param.6, s32[]{:T(128)S(6)} %mul.38), kind=kLoop, calls=%fused_computation.6 | loop fusion | flops 3072 | bytes 12292 | tf_op jit(solution)/shard_map/mul | solution.py:239
  1.4 0.1 copy.11
  1.5 0.2 broadcast_in_dim.41
  1.7 0.3 mul.45
  2.0 0.6 %fusion.3.design_ref = bf16[16,2048]{1,0:T(8,128)(2,1)S(1)} fusion(f32[2048]{0:T(1024)S(1)} %mul.45, f32[16]{0:T(128)S(1)} %fusion.5, pred[16]{0:T(512)(128)(4,1)S(1)} %get-tuple-element.13, pred[16]{0:T(512)(128)(4,1)S(1)} %get-tuple-element.14, pred[16]{0:T(512)(128)(4,1)S(1)} %iota_compare_fusion.1), kind=kLoop, calls=%fused_computation.5 | loop fusion | flops 163840 | bytes 73840 | tf_op jit(solution)/shard_map/convert_element_type | solution.py:25
  2.5 3.0 %prepare.1 = (bf16[544,2048]{1,0:T(8,128)(2,1)S(1)}, f32[16,544]{1,0:T(8,128)S(1)}) custom-call(s32[96,16]{1,0:T(8,128)S(1)} %bitcast.1, bf16[16,2048]{1,0:T(8,128)(2,1)S(1)} %fusion.3.design_ref), custom_call_target="tpu_custom_call" | custom-call | tf_op jit(solution)/shard_map/prepare/pallas_call | solution.py:240
  5.5 38.8 %compose.1 = (f32[8,128,256]{2,1,0:T(8,128)S(1)}, f32[128,256]{1,0:T(8,128)S(1)}) custom-call(bf16[1024,2,2048]{2,1,0:T(2,128)(2,1)} %fields.1, bf16[544,2048]{1,0:T(8,128)(2,1)S(1)} %get-tuple-element.9.weights_hbm, f32[16,544]{1,0:T(8,128)S(1)} %get-tuple-element.10.normal_ref), custom_call_target="tpu_custom_call" | custom-call | tf_op jit(solution)/shard_map/compose/pallas_call | solution.py:253
  44.3 0.0 copy-done
  44.3 2.3 %finish.1 = f32[4,16,2,2048]{3,2,1,0:T(2,128)} custom-call(s32[16]{0:T(128)S(1)} %copy-done, f32[8,128,256]{2,1,0:T(8,128)S(1)} %get-tuple-element.11.values_ref, f32[128,256]{1,0:T(8,128)S(1)} %get-tuple-element.12.mean_ref), custom_call_target="tpu_custom_call" | custom-call | tf_op jit(solution)/shard_map/finish/pallas_call | solution.py:289
  (3 shorter events, 0.0 us)
Async XLA Ops:
  0.0 44.3 %copy-start = (s32[16]{0:T(128)S(1)}, s32[16]{0:T(128)}, u32[]{:S(2)}) copy-start(s32[16]{0:T(128)} %lags_ref.1) | copy-start | bytes 196
